TPU v7x, 256 devices: a whole 4x4x8 slice. The times are simulated.
256 devices in a mesh: level: 4 (over y), blk: 64 (over x, z, core).
Axes of the slice: x: 4, y: 4, z: 8, core: 2. Of those that a mesh axis runs over, the one named last changes fastest.
Arguments:
- right_sides: float32 [4, 512, 16384], P('level', None, 'blk'), may hold values from -6 to 6
- leaf_gen: float32 [4, 16384, 256], P('level', 'blk'), may hold values from -1 to 1, as said below
- leaf_inverse: float32 [4, 8192, 128], P('level', 'blk'), may hold values from -0.5 to 0.5
- leaf_lower: float32 [4, 8192, 128], P('level', 'blk'), may hold values from -0.5 to 0.5
- node_gen: float32 [4, 64, 6, 256, 256], P('level', 'blk'), may hold values from -1 to 1, as said below
- node_inverse: float32 [4, 64, 6, 128, 128], P('level', 'blk'), may hold values from -1 to 1, as said below
- node_lower: float32 [4, 64, 6, 128, 128], P('level', 'blk'), may hold values from -1 to 1, as said below
- coupling: float32 [4, 128, 256], P('level'), may hold values from -0.5 to 0.5
- child_leaf: int32 [4], P('level'), may hold values from 0 to 63
Outputs:
- leaf_solution: float32 [4, 512, 8192], P('level', None, 'blk')
- node_solution: float32 [4, 64, 6, 512, 128], P('level', 'blk')
- root_skeleton: float32 [4, 512, 128], P('level')
Inputs may be any that keep to these rules, and one draw needn't show every extreme that they name: `leaf_gen`: each leaf's 256 x 256 block is orthogonal. node_gen[p, i, h] is orthogonal and equal for all leaves i with the same i >> (h + 1). node_inverse[p, i, h] is equal for all leaves i with the same i >> (h + 1). node_lower[p, i, h] is equal for all leaves i with the same i >> (h + 1).
All inputs are finite; a program needn't handle non-finite values.
Results may differ from a plain program's by a relative error of at most 0.0003.
Values sent between devices are 32-bit elements; how exact they have to be, the bound alone decides.
A program may use at most 64 MiB of HBM per device.

v0:
```python
import jax
import jax.numpy as jnp
from jax import lax
from jax.sharding import Mesh
from jax.sharding import PartitionSpec as P

BLK = ("blk_0", "blk_1", "blk_2")
exact_mode = lax.Precision.HIGHEST


def partner_2(value, axis, distance):
    mask = 2**distance
    pairs = [(source, source ^ mask) for source in range(lax.axis_size(axis))]
    return lax.ppermute(value, axis, pairs)


def from_root(value, axes, root):
    value = jnp.where(lax.axis_index(axes) == root, value, jnp.zeros_like(value))
    for axis in axes:
        value = lax.psum(value, axis)
    return value


def in_one_piece(arrays, axis, dim, along):
    widths = [a.shape[along] for a in arrays]
    both = jnp.concatenate(arrays, axis=along)
    out = lax.all_gather(both, axis, axis=dim, tiled=True)
    return tuple(jnp.split(out, [sum(widths[:k]) for k in range(1, len(widths))], axis=along))


def product(left, right):
    return jnp.matmul(left, right, precision=exact_mode)


def solve_front(
    columns, position, leaf_gen, leaf_inverse, leaf_lower, node_gen, node_inverse, node_lower
):
    redundant = leaf_inverse.shape[2]
    skeleton_size = leaf_lower.shape[2]
    height = node_gen.shape[2]
    turned = product(columns, leaf_gen[0])
    solved = product(turned[:, :redundant], leaf_inverse[0])
    skeleton = turned[:, redundant:] - product(solved, leaf_lower[0])
    node_parts = []
    for tier_index in range(height):
        payload = skeleton
        both = partner_2(payload, BLK, tier_index)
        is_upper = position >> tier_index & 1 == 1
        joined = jnp.where(
            is_upper,
            jnp.concatenate([both, skeleton], axis=1),
            jnp.concatenate([skeleton, both], axis=1),
        )
        generator = node_gen[0, 0, tier_index]
        turned_node = product(joined, generator)
        node_solved = product(turned_node[:, :skeleton_size], node_inverse[0, 0, tier_index])
        skeleton = turned_node[:, skeleton_size:] - product(
            node_solved, node_lower[0, 0, tier_index]
        )
        node_parts.append(node_solved)
    return (solved, jnp.stack(node_parts), skeleton)


def compose_maps(
    position, coupling, leaf_gen, leaf_inverse, leaf_lower, node_gen, node_inverse, node_lower
):
    redundant = leaf_inverse.shape[2]
    skeleton_size = leaf_lower.shape[2]
    height = node_gen.shape[2]
    lifted = product(coupling[0], leaf_gen[0])
    leaf_map = product(lifted[:, :redundant], leaf_inverse[0])
    carried = lifted[:, redundant:] - product(leaf_map, leaf_lower[0])
    tier_maps = []
    for tier_index in range(height):
        is_upper = position >> tier_index & 1 == 1
        generator = node_gen[0, 0, tier_index]
        half_rows = jnp.where(is_upper, generator[skeleton_size:], generator[:skeleton_size])
        turned = product(carried, half_rows)
        node_map = product(turned[:, :skeleton_size], node_inverse[0, 0, tier_index])
        carried = turned[:, skeleton_size:] - product(node_map, node_lower[0, 0, tier_index])
        tier_maps.append(node_map)
    return (leaf_map, jnp.stack(tier_maps), carried)


def shards(
    right_sides,
    leaf_gen,
    leaf_inverse,
    leaf_lower,
    node_gen,
    node_inverse,
    node_lower,
    coupling,
    child_leaf,
):
    column_total = right_sides.shape[1]
    skeleton_size = leaf_lower.shape[2]
    height = node_gen.shape[2]
    level_index = lax.axis_index("level")
    position = lax.axis_index(BLK)
    is_target = position == child_leaf[0]
    tiers = jnp.arange(height, dtype=jnp.int32)
    in_subtree = (position >> tiers + 1 == child_leaf[0] >> tiers + 1)[:, None, None]
    solved, stacked, skeleton = solve_front(
        right_sides[0],
        position,
        leaf_gen,
        leaf_inverse,
        leaf_lower,
        node_gen,
        node_inverse,
        node_lower,
    )
    leaf_map, tier_maps, root_map = compose_maps(
        position, coupling, leaf_gen, leaf_inverse, leaf_lower, node_gen, node_inverse, node_lower
    )
    tier_maps, root_map = (
        from_root(tier_maps, BLK, child_leaf[0]),
        from_root(root_map, BLK, child_leaf[0]),
    )
    all_maps, all_roots = in_one_piece((root_map[None], skeleton[None]), "level", 0, 1)

    def advance(earlier, paired):
        latest = paired[1] + product(earlier, paired[0])
        return (latest, earlier)

    final_root, incomings = lax.scan(
        advance, jnp.zeros((column_total, skeleton_size), jnp.float32), (all_maps, all_roots)
    )
    incoming = lax.dynamic_index_in_dim(incomings, level_index, 0, keepdims=False)
    leaf_part = solved + jnp.where(is_target, product(incoming, leaf_map), 0.0)
    node_part = stacked + jnp.where(in_subtree, product(incoming[None], tier_maps), 0.0)
    root_part = skeleton + product(incoming, root_map)
    return (leaf_part[None], node_part[None, None], root_part[None])


def solution(mesh):
    split = Mesh(
        mesh.devices.reshape(mesh.shape["level"], 4, 8, 2), ("level", "blk_0", "blk_1", "blk_2")
    )
    return jax.shard_map(
        shards,
        mesh=split,
        in_specs=(
            P("level", None, BLK),
            P("level", BLK, None),
            P("level", BLK, None),
            P("level", BLK, None),
            P("level", BLK, None, None, None),
            P("level", BLK, None, None, None),
            P("level", BLK, None, None, None),
            P("level", None, None),
            P("level"),
        ),
        out_specs=(
            P("level", None, BLK),
            P("level", BLK, None, None, None),
            P("level", None, None),
        ),
        check_vma=False,
    )
```

profile of v0, /device:TPU:2, one launch (start us, length us, event | category | flops | bytes accessed | tf_op | source)
XLA Modules:
  0.0 278.1 jit_solution(7446985248511969324)
XLA Ops:
  8.3 1.6 fusion.49
  14.5 1.7 bitcast_dynamic-update-slice_fusion.12
  20.6 1.9 fusion.13
  22.5 2.1 bitcast_dynamic-update-slice_fusion.6
  25.8 1.9 collective-permute-start.1
  27.7 1.7 bitcast_dynamic-update-slice_fusion.8
  29.6 5.4 %collective-permute-done.1 = f32[512,128]{0,1:T(8,128)} collective-permute-done((f32[512,128]{0,1:T(8,128)}, f32[512,128]{0,1:T(8,128)}, u32[]{:S(2)}, u32[]{:S(2)}) %collective-permute-start.1) | collective-permute-done | bytes 262176 | tf_op jit(solution)/shard_map/ppermute | solution.py:14
  35.0 1.9 fusion.19
  36.9 2.1 bitcast_dynamic-update-slice_fusion.5
  40.1 3.3 %collective-permute-start.2 = (f32[512,128]{0,1:T(8,128)}, f32[512,128]{0,1:T(8,128)}, u32[]{:S(2)}, u32[]{:S(2)}) collective-permute-start(f32[512,128]{0,1:T(8,128)} %slice_subtract_fusion.4), channel_id=1, source_target_pairs={{0,4},{1,5},{2,6},{3,7},{4,0},{5,1},{6,2},{7,3},{8,12},{9,13},{10,... | collective-permute-start | bytes 786440 | tf_op jit(solution)/shard_map/ppermute | solution.py:14
  44.3 1.7 bitcast_dynamic-update-slice_fusion.7
  46.0 9.6 %collective-permute-done.2 = f32[512,128]{0,1:T(8,128)} collective-permute-done((f32[512,128]{0,1:T(8,128)}, f32[512,128]{0,1:T(8,128)}, u32[]{:S(2)}, u32[]{:S(2)}) %collective-permute-start.2) | collective-permute-done | bytes 262176 | tf_op jit(solution)/shard_map/ppermute | solution.py:14
  55.5 1.9 fusion.25
  57.4 2.1 bitcast_dynamic-update-slice_fusion.4
  60.7 6.2 %collective-permute-start.3 = (f32[512,128]{0,1:T(8,128)}, f32[512,128]{0,1:T(8,128)}, u32[]{:S(2)}, u32[]{:S(2)}) collective-permute-start(f32[512,128]{0,1:T(8,128)} %slice_subtract_fusion.3), channel_id=1, source_target_pairs={{0,8},{1,9},{2,10},{3,11},{4,12},{5,13},{6,14},{7,15},{8,0},{9,1},... | collective-permute-start | bytes 786440 | tf_op jit(solution)/shard_map/ppermute | solution.py:14
  68.8 10.1 %collective-permute-done.3 = f32[512,128]{0,1:T(8,128)} collective-permute-done((f32[512,128]{0,1:T(8,128)}, f32[512,128]{0,1:T(8,128)}, u32[]{:S(2)}, u32[]{:S(2)}) %collective-permute-start.3) | collective-permute-done | bytes 262176 | tf_op jit(solution)/shard_map/ppermute | solution.py:14
  78.9 1.9 fusion.31
  80.8 2.1 bitcast_dynamic-update-slice_fusion.3
  84.9 28.9 %all-reduce.9.cloned.1.call-done = (f32[128,128]{1,0:T(8,128)}, f32[6,128,128]{2,1,0:T(8,128)}) async-done(((f32[128,128]{1,0:T(8,128)}, f32[6,128,128]{2,1,0:T(8,128)}), (f32[128,128]{1,0:T(8,128)}, f32[6,128,128]{2,1,0:T(8,128)})) %all-reduce.9.cloned.1.call-update) | async-done | bytes 458768 | tf_op jit(solution)/shard_map/psum | solution.py:20
  113.9 1.9 fusion.37
  115.8 2.1 bitcast_dynamic-update-slice_fusion.2
  119.0 2.1 collective-permute-start.5
  121.1 70.3 %all-reduce.7.cloned.1.call-done = (f32[128,128]{1,0:T(8,128)}, f32[6,128,128]{2,1,0:T(8,128)}) async-done(((f32[128,128]{1,0:T(8,128)}, f32[6,128,128]{2,1,0:T(8,128)}), (f32[128,128]{1,0:T(8,128)}, f32[6,128,128]{2,1,0:T(8,128)})) %all-reduce.7.cloned.1.call-update) | async-done | bytes 458768 | tf_op jit(solution)/shard_map/psum | solution.py:20
  191.5 2.0 fusion.43
  193.5 1.9 bitcast_dynamic-update-slice_fusion.1
  196.7 25.2 %all-reduce.11.cloned.1.call-done = (f32[128,128]{1,0:T(8,128)}, f32[6,128,128]{2,1,0:T(8,128)}) async-done(((f32[128,128]{1,0:T(8,128)}, f32[6,128,128]{2,1,0:T(8,128)}), (f32[128,128]{1,0:T(8,128)}, f32[6,128,128]{2,1,0:T(8,128)})) %all-reduce.11.cloned.1.call-update) | async-done | bytes 458768 | tf_op jit(solution)/shard_map/psum | solution.py:20
  223.5 28.8 %all-gather.2.cloned.1.call-done = f32[4,640,128]{2,1,0:T(8,128)} async-done(((f32[1,640,128]{2,1,0:T(8,128)}), f32[4,640,128]{2,1,0:T(8,128)}) %all-gather.2.cloned.1.call-update) | async-done | bytes 1310736 | tf_op jit(solution)/shard_map/all_gather | solution.py:27
  252.3 1.8 split.9
  254.1 8.8 %while.13 = (s32[]{:T(128)}, f32[512,128]{0,1:T(8,128)S(1)}, f32[4,512,128]{1,2,0:T(8,128)}, f32[4,512,128]{2,1,0:T(8,128)S(1)}, f32[4,128,128]{2,1,0:T(8,128)}, /*index=5*/s32[]{:T(128)}, s32[]{:T(128)}) while((s32[]{:T(128)}, f32[512,128]{0,1:T(8,128)S(1)}, f32[4,512,128]{1,2,0:T(8,128)}, f32[4,512,128]{2,1,0:T(8,128)S(1)}, ...), condition=%wide.region_4.5_spmd.clone, body=%wide.region_3.4_spmd.clone.sunk | while | flops 100859904 | bytes 2949228 | solution.py:127
  262.9 2.3 fusion.9
  265.2 2.2 fusion.11
  267.4 4.1 %fusion.8 = f32[1,1,6,512,128]{4,3,2,1,0:T(8,128)} fusion(f32[6,512,128]{2,1,0:T(8,128)} %get-tuple-element.97, f32[6,128,128]{2,1,0:T(8,128)S(1)} %copy-done.4, pred[6]{0:T(512)(128)(4,1)S(1)} %shift-right-arithmetic_compare_fusion, f32[4,512,128]{1,2,0:T(8,128)} %get-tuple-element.30, s32[]{:T(128)S(6)} %select_n.162), kind=kOutput, calls=%fused_computation.12 | convolution fusion | flops 604766208 | bytes 3801098 | tf_op jit(solution)/shard_map/dot_general | solution.py:32
  (85 shorter events, 30.3 us)
Async XLA Ops:
  7.2 1.1 copy-start
  7.2 6.7 %copy-start.5 = (f32[1,128,128]{2,1,0:T(8,128)S(1)}, f32[1,128,128]{2,1,0:T(8,128)}, u32[]{:S(2)}) copy-start(f32[1,128,128]{2,1,0:T(8,128)} %param.13) | copy-start | bytes 196612
  7.2 4.2 %copy-start.7 = (f32[1,128,128]{2,1,0:T(8,128)S(1)}, f32[1,128,128]{2,1,0:T(8,128)}, u32[]{:S(2)}) copy-start(f32[1,128,128]{2,1,0:T(8,128)} %param.14) | copy-start | bytes 196612
  7.2 5.3 %copy-start.8 = (f32[1,128,256]{2,1,0:T(8,128)S(1)}, f32[1,128,256]{2,1,0:T(8,128)}, u32[]{:S(2)}) copy-start(f32[1,128,256]{2,1,0:T(8,128)} %param.18) | copy-start | bytes 393220
  7.2 7.1 %copy-start.1 = (f32[1,1,6,256,256]{4,3,2,1,0:T(8,128)S(1)}, f32[1,1,6,256,256]{4,3,2,1,0:T(8,128)}, u32[]{:S(2)}) copy-start(f32[1,1,6,256,256]{4,3,2,1,0:T(8,128)} %param.15) | copy-start | bytes 4718596
  7.2 106.6 %all-reduce.9.cloned.1.call-start = ((), (), s32[]{:S(2)}) async-start(), calls=%async_computation.2 | async-start | bytes 917504 | tf_op jit(solution)/shard_map/psum | solution.py:20
  9.9 6.3 %copy-start.2 = (f32[1,1,6,128,128]{4,3,2,1,0:T(8,128)S(1)}, f32[1,1,6,128,128]{4,3,2,1,0:T(8,128)}, u32[]{:S(2)}) copy-start(f32[1,1,6,128,128]{4,3,2,1,0:T(8,128)} %param.17) | copy-start | bytes 1179652
  12.5 4.2 %copy-start.3 = (f32[1,1,6,128,128]{4,3,2,1,0:T(8,128)S(1)}, f32[1,1,6,128,128]{4,3,2,1,0:T(8,128)}, u32[]{:S(2)}) copy-start(f32[1,1,6,128,128]{4,3,2,1,0:T(8,128)} %param.16) | copy-start | bytes 1179652
  12.5 8.1 %collective-permute-start = (f32[512,128]{0,1:T(8,128)}, f32[512,128]{0,1:T(8,128)}, u32[]{:S(2)}, u32[]{:S(2)}) collective-permute-start(f32[512,128]{0,1:T(8,128)} %convolution_subtract_fusion), channel_id=1, source_target_pairs={{0,1},{1,0},{2,3},{3,2},{4,5},{5,4},{6,7},{7,6},{8,9},{9,8},{10,11... | collective-permute-start | bytes 786440 | tf_op jit(solution)/shard_map/ppermute | solution.py:14
  25.8 9.2 %collective-permute-start.1 = (f32[512,128]{0,1:T(8,128)}, f32[512,128]{0,1:T(8,128)}, u32[]{:S(2)}, u32[]{:S(2)}) collective-permute-start(f32[512,128]{0,1:T(8,128)} %slice_subtract_fusion.5), channel_id=1, source_target_pairs={{0,2},{1,3},{2,0},{3,1},{4,6},{5,7},{6,4},{7,5},{8,10},{9,11},{10,... | collective-permute-start | bytes 786440 | tf_op jit(solution)/shard_map/ppermute | solution.py:14
  40.1 15.4 %collective-permute-start.2 = (f32[512,128]{0,1:T(8,128)}, f32[512,128]{0,1:T(8,128)}, u32[]{:S(2)}, u32[]{:S(2)}) collective-permute-start(f32[512,128]{0,1:T(8,128)} %slice_subtract_fusion.4), channel_id=1, source_target_pairs={{0,4},{1,5},{2,6},{3,7},{4,0},{5,1},{6,2},{7,3},{8,12},{9,13},{10,... | collective-permute-start | bytes 786440 | tf_op jit(solution)/shard_map/ppermute | solution.py:14
  60.7 18.3 %collective-permute-start.3 = (f32[512,128]{0,1:T(8,128)}, f32[512,128]{0,1:T(8,128)}, u32[]{:S(2)}, u32[]{:S(2)}) collective-permute-start(f32[512,128]{0,1:T(8,128)} %slice_subtract_fusion.3), channel_id=1, source_target_pairs={{0,8},{1,9},{2,10},{3,11},{4,12},{5,13},{6,14},{7,15},{8,0},{9,1},... | collective-permute-start | bytes 786440 | tf_op jit(solution)/shard_map/ppermute | solution.py:14
  68.6 122.8 %all-reduce.7.cloned.1.call-start = ((), (), s32[]{:S(2)}) async-start(), calls=%async_computation.1 | async-start | bytes 917504 | tf_op jit(solution)/shard_map/psum | solution.py:20
  84.1 29.8 %collective-permute-start.4 = (f32[512,128]{0,1:T(8,128)}, f32[512,128]{0,1:T(8,128)}, u32[]{:S(2)}, u32[]{:S(2)}) collective-permute-start(f32[512,128]{0,1:T(8,128)} %slice_subtract_fusion.2), channel_id=1, source_target_pairs={{0,16},{1,17},{2,18},{3,19},{4,20},{5,21},{6,22},{7,23},{8,24},{9,... | collective-permute-start | bytes 786440 | tf_op jit(solution)/shard_map/ppermute | solution.py:14
  113.8 108.0 %all-reduce.11.cloned.1.call-start = ((), (), s32[]{:S(2)}) async-start(), calls=%async_computation.3 | async-start | bytes 917504 | tf_op jit(solution)/shard_map/psum | solution.py:20
  119.0 72.4 %collective-permute-start.5 = (f32[512,128]{0,1:T(8,128)}, f32[512,128]{0,1:T(8,128)S(1)}, u32[]{:S(2)}, u32[]{:S(2)}) collective-permute-start(f32[512,128]{0,1:T(8,128)} %slice_subtract_fusion.1), channel_id=1, source_target_pairs={{0,32},{1,33},{2,34},{3,35},{4,36},{5,37},{6,38},{7,39},{8,40},{9,... | collective-permute-start | bytes 786440 | tf_op jit(solution)/shard_map/ppermute | solution.py:14
  191.4 60.9 %all-gather.2.cloned.1.call-start = ((), (), s32[]{:S(2)}) async-start(), calls=%async_computation | async-start | bytes 1638400 | tf_op jit(solution)/shard_map/all_gather | solution.py:27
  252.3 1.8 slice-start
  254.1 8.8 %copy-start.6 = (f32[128,128]{1,0:T(8,128)S(1)}, f32[128,128]{1,0:T(8,128)}, u32[]{:S(2)}) copy-start(f32[128,128]{1,0:T(8,128)} %get-tuple-element.73) | copy-start | bytes 196612
  262.9 4.6 %copy-start.4 = (f32[6,128,128]{2,1,0:T(8,128)S(1)}, f32[6,128,128]{2,1,0:T(8,128)}, u32[]{:S(2)}) copy-start(f32[6,128,128]{2,1,0:T(8,128)} %get-tuple-element.74) | copy-start | bytes 1179652
Sparse Core Ops, SparseCore 0:
  68.7 45.1 all-reduce.8
  116.2 75.1 all-reduce.6
  194.1 27.7 all-reduce.10
  223.6 28.6 all-gather.1
where the time goes:
time: 279 us; the launch traced here: 278 us
  waiting for transfers between devices  178 us (64%)
  matrix products  61.2 us (22%)
  between operations  14.8 us (5%)
  starting transfers between devices  14.7 us (5%)
  other arithmetic  5.31 us (2%)
  local copies, waits for them, and re-layouts  3.54 us (1%)
    psum x3, waiting for transfers between devices, from_root(): value = lax.psum(value, axis)  124 us
    dot_general x49, matrix products, product(): return jnp.matmul(left, right, precision=exact_mode)  61.2 us
    all_gather x1, waiting for transfers between devices, in_one_piece(): out = lax.all_gather(both, axis, axis=dim, tiled=True)  28.8 us
    ppermute x6, waiting for transfers between devices, partner_2(): return lax.ppermute(value, axis, pairs)  25.1 us
    ppermute x6, starting transfers between devices, partner_2(): return lax.ppermute(value, axis, pairs)  14.3 us
  transfers between devices with their start and end apart: 10, of which 7 were waited for; matrix products, arithmetic and copies ran while one was open for 10% of the time, Pallas kernels for 0%

commit v1 on v0

--- a/solution.py
+++ b/solution.py
@@ -17,7 +17,8 @@
 def from_root(value, axes, root):
     value = jnp.where(lax.axis_index(axes) == root, value, jnp.zeros_like(value))
     for axis in axes:
-        value = lax.psum(value, axis)
+        blocks = lax.all_gather(value, axis, axis=0, tiled=False)
+        value = blocks.sum(axis=0)
     return value
 
 

time: 279 us -> 236 us (0.85)
  waiting for transfers between devices: 178 us -> 81.8 us
  blocking collectives: 0 us -> 50.6 us
  other arithmetic: 5.31 us -> 8.99 us
    psum x3 -> x0, waiting for transfers between devices: 124 us -> none  [from_root(): value = lax.psum(value, axis)]
    all_gather x0 -> x4, blocking collectives: none -> 50.6 us  [from_root(): blocks = lax.all_gather(value, axis, axis=0, tiled=False)]
    all_gather x0 -> x2, waiting for transfers between devices: none -> 32.3 us  [from_root(): blocks = lax.all_gather(value, axis, axis=0, tiled=False)]
    all_gather x1, waiting for transfers between devices: 28.8 us -> 24.1 us  [in_one_piece(): out = lax.all_gather(both, axis, axis=dim, tiled=True)]
    reduce_sum x0 -> x6, other arithmetic: none -> 4.47 us  [from_root(): value = blocks.sum(axis=0)]
  transfers between devices with their start and end apart: 10 -> 9, of which waited for: 7 -> 5; matrix products, arithmetic and copies ran while one was open for 10% -> 20% of each run, Pallas kernels for 0% -> 0%
where the time goes in v1:
time: 236 us; the launch traced here: 233 us
  waiting for transfers between devices  81.8 us (35%)
  matrix products  58.8 us (25%)
  blocking collectives  50.6 us (21%)
  between operations  14.8 us (6%)
  starting transfers between devices  14.7 us (6%)
  other arithmetic  8.99 us (4%)
  local copies, waits for them, and re-layouts  3.48 us (1%)
    dot_general x49, matrix products, product(): return jnp.matmul(left, right, precision=exact_mode)  58.8 us
    all_gather x4, blocking collectives, from_root(): blocks = lax.all_gather(value, axis, axis=0, tiled=False)  50.6 us
    all_gather x2, waiting for transfers between devices, from_root(): blocks = lax.all_gather(value, axis, axis=0, tiled=False)  32.3 us
    ppermute x6, waiting for transfers between devices, partner_2(): return lax.ppermute(value, axis, pairs)  25.3 us
    all_gather x1, waiting for transfers between devices, in_one_piece(): out = lax.all_gather(both, axis, axis=dim, tiled=True)  24.1 us
    ppermute x6, starting transfers between devices, partner_2(): return lax.ppermute(value, axis, pairs)  14.4 us
  transfers between devices with their start and end apart: 9, of which 5 were waited for; matrix products, arithmetic and copies ran while one was open for 20% of the time, Pallas kernels for 0%

profile of v1, /device:TPU:2, one launch (start us, length us, event | category | flops | bytes accessed | tf_op | source)
XLA Modules:
  0.0 233.4 jit_solution(3022345347344726104)
XLA Ops:
  20.4 1.9 fusion.13
  22.3 2.1 bitcast_dynamic-update-slice_fusion.6
  24.8 2.0 collective-permute-start.1
  28.8 5.0 %collective-permute-done.1 = f32[512,128]{0,1:T(8,128)S(1)} collective-permute-done((f32[512,128]{0,1:T(8,128)S(1)}, f32[512,128]{0,1:T(8,128)S(1)}, u32[]{:S(2)}, u32[]{:S(2)}) %collective-permute-start.1) | collective-permute-done | bytes 262176 | tf_op jit(solution)/shard_map/ppermute | solution.py:14
  34.5 2.1 bitcast_dynamic-update-slice_fusion.5
  37.7 3.3 %collective-permute-start.2 = (f32[512,128]{0,1:T(8,128)}, f32[512,128]{0,1:T(8,128)}, u32[]{:S(2)}, u32[]{:S(2)}) collective-permute-start(f32[512,128]{0,1:T(8,128)} %slice_subtract_fusion.4), channel_id=1, source_target_pairs={{0,4},{1,5},{2,6},{3,7},{4,0},{5,1},{6,2},{7,3},{8,12},{9,13},{10,... | collective-permute-start | bytes 786440 | tf_op jit(solution)/shard_map/ppermute | solution.py:14
  41.5 11.7 %collective-permute-done.2 = f32[512,128]{0,1:T(8,128)} collective-permute-done((f32[512,128]{0,1:T(8,128)}, f32[512,128]{0,1:T(8,128)}, u32[]{:S(2)}, u32[]{:S(2)}) %collective-permute-start.2) | collective-permute-done | bytes 262176 | tf_op jit(solution)/shard_map/ppermute | solution.py:14
  53.2 1.9 fusion.25
  55.1 2.1 bitcast_dynamic-update-slice_fusion.4
  58.3 6.2 %collective-permute-start.3 = (f32[512,128]{0,1:T(8,128)}, f32[512,128]{0,1:T(8,128)}, u32[]{:S(2)}, u32[]{:S(2)}) collective-permute-start(f32[512,128]{0,1:T(8,128)} %slice_subtract_fusion.3), channel_id=1, source_target_pairs={{0,8},{1,9},{2,10},{3,11},{4,12},{5,13},{6,14},{7,15},{8,0},{9,1},... | collective-permute-start | bytes 786440 | tf_op jit(solution)/shard_map/ppermute | solution.py:14
  64.5 1.7 bitcast_dynamic-update-slice_fusion.7
  67.9 8.6 %collective-permute-done.3 = f32[512,128]{0,1:T(8,128)} collective-permute-done((f32[512,128]{0,1:T(8,128)}, f32[512,128]{0,1:T(8,128)}, u32[]{:S(2)}, u32[]{:S(2)}) %collective-permute-start.3) | collective-permute-done | bytes 262176 | tf_op jit(solution)/shard_map/ppermute | solution.py:14
  76.6 1.9 fusion.31
  78.5 2.1 bitcast_dynamic-update-slice_fusion.3
  82.8 21.0 %all-gather = f32[512,128]{1,0:T(8,128)S(1)} all-gather(f32[128,128]{1,0:T(8,128)S(1)} %fusion.12), channel_id=2, replica_groups=mesh['level'=4,'blk_0'=4,'blk_1'=8,'blk_2'=2] {'blk_0'}, dimensions={0}, use_global_device_ids=true | all-gather | bytes 327680 | tf_op jit(solution)/shard_map/all_gather | solution.py:20
  103.8 1.9 fusion.37
  105.7 2.1 bitcast_dynamic-update-slice_fusion.2
  109.0 2.1 collective-permute-start.5
  111.0 25.4 %all-gather.1 = f32[1024,128]{1,0:T(8,128)S(1)} all-gather(f32[128,128]{1,0:T(8,128)S(1)} %reduce_sum.54), channel_id=3, replica_groups=mesh['level'=4,'blk_0'=4,'blk_1'=8,'blk_2'=2] {'blk_1'}, dimensions={0}, use_global_device_ids=true | all-gather | bytes 589824 | tf_op jit(solution)/shard_map/all_gather | solution.py:20
  136.5 1.9 all-gather.2
  138.4 2.0 fusion.43
  140.4 1.9 bitcast_dynamic-update-slice_fusion.1
  144.4 2.3 reduce_sum.57
  146.8 24.1 %all-gather.9.cloned.1.call-done = f32[4,640,128]{2,1,0:T(8,128)} async-done(((f32[1,640,128]{2,1,0:T(8,128)}), f32[4,640,128]{2,1,0:T(8,128)}) %all-gather.9.cloned.1.call-update) | async-done | bytes 1310736 | tf_op jit(solution)/shard_map/all_gather | solution.py:28
  170.9 1.8 split.9
  172.6 8.8 %while.13 = (s32[]{:T(128)}, f32[512,128]{0,1:T(8,128)S(1)}, f32[4,512,128]{1,2,0:T(8,128)}, f32[4,512,128]{2,1,0:T(8,128)S(1)}, f32[4,128,128]{2,1,0:T(8,128)}, /*index=5*/s32[]{:T(128)}, s32[]{:T(128)}) while((s32[]{:T(128)}, f32[512,128]{0,1:T(8,128)S(1)}, f32[4,512,128]{1,2,0:T(8,128)}, f32[4,512,128]{2,1,0:T(8,128)S(1)}, ...), condition=%wide.region_4.5_spmd.clone, body=%wide.region_3.4_spmd.clone.sunk | while | flops 100859904 | bytes 2949228 | solution.py:128
  181.5 2.2 fusion.11
  183.7 2.2 fusion.9
  186.0 32.3 %all-gather.13.cloned.1.call-done = f32[48,128,128]{2,1,0:T(8,128)} async-done(((f32[6,128,128]{2,1,0:T(8,128)}), f32[48,128,128]{2,1,0:T(8,128)}) %all-gather.13.cloned.1.call-update) | async-done | bytes 3145744 | tf_op jit(solution)/shard_map/all_gather | solution.py:20
  218.3 2.1 reduce_sum.58
  220.3 2.4 %all-gather.4 = f32[12,128,128]{2,1,0:T(8,128)S(1)} all-gather(f32[6,128,128]{2,1,0:T(8,128)S(1)} %reduce_sum.58), channel_id=6, replica_groups=mesh['level'=4,'blk_0'=4,'blk_1'=8,'blk_2'=2] {'blk_2'}, dimensions={0}, use_global_device_ids=true | all-gather | bytes 1179648 | tf_op jit(solution)/shard_map/all_gather | solution.py:20
  222.8 4.1 %fusion.8 = f32[1,1,6,512,128]{4,3,2,1,0:T(8,128)} fusion(f32[6,512,128]{2,1,0:T(8,128)} %get-tuple-element.84, f32[6,128,128]{2,1,0:T(8,128)S(1)} %reduce_sum.59, pred[6]{0:T(512)(128)(4,1)S(1)} %shift-right-arithmetic_compare_fusion, f32[4,512,128]{1,2,0:T(8,128)} %get-tuple-element.30, s32[]{:T(128)S(6)} %select_n.169), kind=kOutput, calls=%fused_computation.12 | convolution fusion | flops 604766208 | bytes 3801098 | tf_op jit(solution)/shard_map/dot_general | solution.py:33
  (88 shorter events, 33.9 us)
Async XLA Ops:
  7.2 1.1 copy-start
  7.2 6.6 %copy-start.4 = (f32[1,128,128]{2,1,0:T(8,128)S(1)}, f32[1,128,128]{2,1,0:T(8,128)}, u32[]{:S(2)}) copy-start(f32[1,128,128]{2,1,0:T(8,128)} %param.13) | copy-start | bytes 196612
  7.2 4.2 %copy-start.6 = (f32[1,128,128]{2,1,0:T(8,128)S(1)}, f32[1,128,128]{2,1,0:T(8,128)}, u32[]{:S(2)}) copy-start(f32[1,128,128]{2,1,0:T(8,128)} %param.14) | copy-start | bytes 196612
  7.2 7.1 %copy-start.1 = (f32[1,1,6,256,256]{4,3,2,1,0:T(8,128)S(1)}, f32[1,1,6,256,256]{4,3,2,1,0:T(8,128)}, u32[]{:S(2)}) copy-start(f32[1,1,6,256,256]{4,3,2,1,0:T(8,128)} %param.15) | copy-start | bytes 4718596
  7.2 137.2 %all-gather.11.cloned.1.call-start = ((), (), s32[]{:S(2)}) async-start(), calls=%async_computation.1 | async-start | bytes 1966080 | tf_op jit(solution)/shard_map/all_gather | solution.py:20
  9.8 6.4 %copy-start.2 = (f32[1,1,6,128,128]{4,3,2,1,0:T(8,128)S(1)}, f32[1,1,6,128,128]{4,3,2,1,0:T(8,128)}, u32[]{:S(2)}) copy-start(f32[1,1,6,128,128]{4,3,2,1,0:T(8,128)} %param.17) | copy-start | bytes 1179652
  12.5 4.2 %copy-start.3 = (f32[1,1,6,128,128]{4,3,2,1,0:T(8,128)S(1)}, f32[1,1,6,128,128]{4,3,2,1,0:T(8,128)}, u32[]{:S(2)}) copy-start(f32[1,1,6,128,128]{4,3,2,1,0:T(8,128)} %param.16) | copy-start | bytes 1179652
  12.5 7.9 %collective-permute-start = (f32[512,128]{0,1:T(8,128)}, f32[512,128]{0,1:T(8,128)}, u32[]{:S(2)}, u32[]{:S(2)}) collective-permute-start(f32[512,128]{0,1:T(8,128)} %convolution_subtract_fusion), channel_id=1, source_target_pairs={{0,1},{1,0},{2,3},{3,2},{4,5},{5,4},{6,7},{7,6},{8,9},{9,8},{10,11... | collective-permute-start | bytes 786440 | tf_op jit(solution)/shard_map/ppermute | solution.py:14
  24.8 8.9 %collective-permute-start.1 = (f32[512,128]{0,1:T(8,128)S(1)}, f32[512,128]{0,1:T(8,128)S(1)}, u32[]{:S(2)}, u32[]{:S(2)}) collective-permute-start(f32[512,128]{0,1:T(8,128)S(1)} %slice_subtract_fusion.5), channel_id=1, source_target_pairs={{0,2},{1,3},{2,0},{3,1},{4,6},{5,7},{6,4},{7,5},{8,10},{9,11},{10,... | collective-permute-start | bytes 786440 | tf_op jit(solution)/shard_map/ppermute | solution.py:14
  37.7 15.4 %collective-permute-start.2 = (f32[512,128]{0,1:T(8,128)}, f32[512,128]{0,1:T(8,128)}, u32[]{:S(2)}, u32[]{:S(2)}) collective-permute-start(f32[512,128]{0,1:T(8,128)} %slice_subtract_fusion.4), channel_id=1, source_target_pairs={{0,4},{1,5},{2,6},{3,7},{4,0},{5,1},{6,2},{7,3},{8,12},{9,13},{10,... | collective-permute-start | bytes 786440 | tf_op jit(solution)/shard_map/ppermute | solution.py:14
  58.3 18.2 %collective-permute-start.3 = (f32[512,128]{0,1:T(8,128)}, f32[512,128]{0,1:T(8,128)}, u32[]{:S(2)}, u32[]{:S(2)}) collective-permute-start(f32[512,128]{0,1:T(8,128)} %slice_subtract_fusion.3), channel_id=1, source_target_pairs={{0,8},{1,9},{2,10},{3,11},{4,12},{5,13},{6,14},{7,15},{8,0},{9,1},... | collective-permute-start | bytes 786440 | tf_op jit(solution)/shard_map/ppermute | solution.py:14
  67.7 103.2 %all-gather.9.cloned.1.call-start = ((), (), s32[]{:S(2)}) async-start(), calls=%async_computation | async-start | bytes 1638400 | tf_op jit(solution)/shard_map/all_gather | solution.py:28
  67.9 14.7 %copy-start.5 = (f32[128,128]{1,0:T(8,128)S(1)}, f32[128,128]{1,0:T(8,128)}, u32[]{:S(2)}) copy-start(f32[128,128]{1,0:T(8,128)} %get-tuple-element.97) | copy-start | bytes 196612
  81.7 22.1 %collective-permute-start.4 = (f32[512,128]{0,1:T(8,128)}, f32[512,128]{0,1:T(8,128)}, u32[]{:S(2)}, u32[]{:S(2)}) collective-permute-start(f32[512,128]{0,1:T(8,128)} %slice_subtract_fusion.2), channel_id=1, source_target_pairs={{0,16},{1,17},{2,18},{3,19},{4,20},{5,21},{6,22},{7,23},{8,24},{9,... | collective-permute-start | bytes 786440 | tf_op jit(solution)/shard_map/ppermute | solution.py:14
  109.0 29.4 %collective-permute-start.5 = (f32[512,128]{0,1:T(8,128)}, f32[512,128]{0,1:T(8,128)S(1)}, u32[]{:S(2)}, u32[]{:S(2)}) collective-permute-start(f32[512,128]{0,1:T(8,128)} %slice_subtract_fusion.1), channel_id=1, source_target_pairs={{0,32},{1,33},{2,34},{3,35},{4,36},{5,37},{6,38},{7,39},{8,40},{9,... | collective-permute-start | bytes 786440 | tf_op jit(solution)/shard_map/ppermute | solution.py:14
  144.4 73.9 %all-gather.13.cloned.1.call-start = ((), (), s32[]{:S(2)}) async-start(), calls=%async_computation.2 | async-start | bytes 3538944 | tf_op jit(solution)/shard_map/all_gather | solution.py:20
  170.9 1.8 slice-start
Sparse Core Ops, SparseCore 0:
  67.8 31.2 all-gather.10
  144.5 26.3 all-gather.8
  172.7 45.5 all-gather.12
